TPU v7x, 32 devices: a whole 2x2x4 slice. The times are simulated.
32 devices in a mesh: space: 16 (over z, x, core), chan: 2 (over y).
Axes of the slice: x: 2, y: 2, z: 4, core: 2. Of those that a mesh axis runs over, the one named last changes fastest.
Arguments:
- inputs: bfloat16 [64, 32, 64, 128], P('chan', 'space'), may hold values from -6 to 6
- grad_out: bfloat16 [64, 32, 64, 128], P('chan', 'space'), may hold values from -6 to 6
- filt: bfloat16 [27, 64, 64], P(None, 'chan'), may hold values from -0.15625 to 0.15625
Outputs:
- grad_inputs: bfloat16 [64, 32, 64, 128], P('chan', 'space')
- grad_filt: float32 [27, 64, 64], P(None, 'chan', 'space')
All inputs are finite; a program needn't handle non-finite values.
Results may differ from a plain program's by a relative error of at most 0.0066.
Values may be sent and summed in bfloat16 or wider, within the bound.
A program may use at most 128 MiB of HBM per device.

v0:
```python
import functools

import jax
import jax.numpy as jnp
from jax import lax
from jax.experimental import pallas as pl
from jax.experimental.pallas import tpu as pltpu
from jax.sharding import PartitionSpec as P


def with_halo(x, sides, width):
    for axis, dim in sides:
        size, length = (lax.axis_size(axis), x.shape[dim])
        up = [(i, (i + 1) % size) for i in range(size - 1)]
        down = [(j, i) for i, j in up]
        last = lax.slice_in_dim(x, length - width, length, axis=dim)
        first = lax.slice_in_dim(x, 0, width, axis=dim)
        before = lax.ppermute(last, axis, up)
        after = lax.ppermute(first, axis, down)
        x = jnp.concatenate([before, x, after], axis=dim)
    return x


def columns(field):
    padded = jnp.pad(field, ((0, 0), (0, 0), (1, 1), (1, 1)))
    height = field.shape[2]
    row_len = field.shape[3]
    shifted = []
    for tap_row in range(3):
        for tap_col in range(3):
            shifted.append(
                padded[
                    :, :, 2 - tap_row : 2 - tap_row + height, 2 - tap_col : 2 - tap_col + row_len
                ]
            )
    return jnp.concatenate(shifted, axis=0)


def flat_window(field, first, planes):
    window = lax.slice_in_dim(field, first, first + planes, axis=1)
    return window.reshape(window.shape[0], -1)


def local(inputs, grad_out, filt):
    planes = inputs.shape[1]
    height = inputs.shape[2]
    row_len = inputs.shape[3]
    out_local = grad_out.shape[0]
    chan_total = filt.shape[2]
    tap_rows = 9 * out_local
    kernel = filt.reshape(3, tap_rows, chan_total)
    shifted_out = with_halo(grad_out, (("space", 1),), 1)
    stacked = columns(shifted_out)
    grad_left = [flat_window(stacked, 2 - depth_tap, planes) for depth_tap in range(3)]
    source_first = [0, 0, 0]
    segment = lax.all_gather(inputs, "chan", axis=0, tiled=True)
    blocks = []
    for depth_tap in range(3):
        right_side = flat_window(segment, source_first[depth_tap], planes)
        blocks.append(
            lax.dot_general(
                grad_left[depth_tap],
                right_side,
                (((1,), (1,)), ((), ())),
                preferred_element_type=jnp.float32,
            )
        )
    update = jnp.stack(blocks, 0)
    grad_filt = lax.psum_scatter(
        update.reshape(27, out_local, chan_total), "space", scatter_dimension=2, tiled=True
    )
    own_rows = chan_total // lax.axis_size("chan")
    total = None
    for depth_tap in range(3):
        product = lax.dot_general(
            kernel[depth_tap],
            grad_left[depth_tap],
            (((0,), (0,)), ((), ())),
            preferred_element_type=jnp.float32,
        )
        product = product.reshape(lax.axis_size("chan") * own_rows, planes, height, row_len)
        total = product if total is None else total + product
    summed = lax.psum_scatter(total, "chan", scatter_dimension=0, tiled=True)
    return (summed.astype(jnp.bfloat16), grad_filt)


ROWS = 16


def place(at, rel, size):
    return lax.rem(at + rel, size)


def body(
    n_space,
    n_chan,
    filt_ref,
    in_ref,
    out_hbm,
    gi_ref,
    gf_ref,
    raw,
    cols,
    source,
    held,
    total,
    weights,
    their_filt,
    sums,
    leave,
    land,
    own_sem,
    y_send,
    h_send,
    arrive,
    f_send,
    f_recv,
    s_send,
    s_recv,
):
    mine = in_ref.shape[0]
    height, width = in_ref.shape[2], in_ref.shape[3]
    chunks = height // ROWS
    group = 4 * mine
    s = lax.axis_index("space")
    k = lax.axis_index("chan")
    lane = lax.broadcasted_iota(jnp.int32, (mine, width), 1)

    def rows_of(c):
        return pl.ds(c * ROWS, ROWS)

    def y_copy(rel, plane, c):
        return pltpu.make_async_remote_copy(
            src_ref=out_hbm.at[:, plane, rows_of(c), :],
            dst_ref=raw.at[n_chan - rel, plane + 1, :, rows_of(c), :],
            send_sem=y_send.at[rel - 1, plane, c],
            recv_sem=arrive.at[n_chan - rel, plane + 1, c],
            device_id=(s, place(k, rel, n_chan)),
            device_id_type=pl.DeviceIdType.MESH,
        )

    def halo_copy(rel, side, c):
        if rel == 0:
            src = out_hbm.at[:, side, rows_of(c), :]
        else:
            src = raw.at[rel, side + 1, :, rows_of(c), :]
        land_plane = 3 if side == 0 else 0
        other = lax.max(s - 1, 0) if side == 0 else lax.min(s + 1, n_space - 1)
        return pltpu.make_async_remote_copy(
            src_ref=src,
            dst_ref=raw.at[rel, land_plane, :, rows_of(c), :],
            send_sem=h_send.at[rel, side, c],
            recv_sem=arrive.at[rel, land_plane, c],
            device_id=(other, k),
            device_id_type=pl.DeviceIdType.MESH,
        )

    def filt_copy(rel):
        return pltpu.make_async_remote_copy(
            src_ref=filt_ref.at[place(k, rel, n_chan)],
            dst_ref=their_filt.at[n_chan - rel],
            send_sem=f_send.at[rel - 1],
            recv_sem=f_recv.at[n_chan - rel - 1],
            device_id=(s, place(k, rel, n_chan)),
            device_id_type=pl.DeviceIdType.MESH,
        )

    def own_copy(plane):
        return pltpu.make_async_copy(
            out_hbm.at[:, plane], raw.at[0, plane + 1], own_sem.at[plane]
        )

    below, above = s > 0, s < n_space - 1

    def send_halo(rel, c):
        @pl.when(below)
        def _():
            halo_copy(rel, 0, c).start()

        @pl.when(above)
        def _():
            halo_copy(rel, 1, c).start()

    for rel in range(1, n_chan):
        filt_copy(rel).start()
    for c in range(chunks):
        for rel in range(1, n_chan):
            for plane in range(2):
                y_copy(rel, plane, c).start()
        send_halo(0, c)
    for plane in range(2):
        own_copy(plane).start()

    pad = jnp.zeros((source.shape[0], width), jnp.bfloat16)
    source[:, 0:width] = pad
    source[:, (height + 1) * width : (height + 2) * width] = pad
    pad = jnp.zeros((cols.shape[0], width), jnp.bfloat16)
    cols[:, 0:width] = pad
    cols[:, (height + 1) * width : (height + 2) * width] = pad

    def source_step(c, carry):
        first = pl.multiple_of(c * ROWS, ROWS)
        for plane in range(2):
            block = in_ref[:, plane, pl.ds(first, ROWS), :].astype(jnp.float32)
            held[...] = block.reshape(mine * ROWS, width)
            for h in range(ROWS):
                row = held[pl.ds(h, mine, stride=ROWS), :]
                left = jnp.where(lane > 0, pltpu.roll(row, 1, 1), 0.0)
                right = jnp.where(lane < width - 1, pltpu.roll(row, width - 1, 1), 0.0)
                at = pl.ds(pl.multiple_of((first + h + 1) * width, width), width)
                for e, value in enumerate((left, row, right)):
                    top = (2 * e + plane) * mine
                    source[top : top + mine, at] = value.astype(jnp.bfloat16)
        return carry

    lax.fori_loop(0, chunks, source_step, 0)

    def set_weights(rel, value):
        taps = value.astype(jnp.float32)
        moved = pltpu.roll(taps, mine, 1)
        for b in range(3):
            for e in range(3):
                at = (3 * b + e) * mine
                top = 2 * e * mine
                span = slice(rel * group, (rel + 1) * group)
                weights[b, top : top + mine, span] = taps[at : at + mine].astype(jnp.bfloat16)
                weights[b, top + mine : top + 2 * mine, span] = moved[at : at + mine].astype(
                    jnp.bfloat16
                )

    set_weights(0, filt_ref[k])
    for rel in range(1, n_chan):
        filt_copy(rel).wait()
    for rel in range(1, n_chan):
        set_weights(rel, their_filt[rel])

    def lay(rel, plane, c):
        block = raw[rel, plane, :, rows_of(c), :].astype(jnp.float32)
        held[...] = block.reshape(mine * ROWS, width)
        top = rel * group + plane * mine
        for h in range(ROWS):
            row = held[pl.ds(h, mine, stride=ROWS), :]
            at = (c * ROWS + h + 1) * width
            cols[top : top + mine, at : at + width] = row.astype(jnp.bfloat16)

    def lay_halo(rel, side, c):
        plane = 0 if side == 1 else 3
        there = below if side == 1 else above

        @pl.when(there)
        def _():
            halo_copy(rel, side, c).wait_recv()
            lay(rel, plane, c)

        @pl.when(jnp.logical_not(there))
        def _():
            top = rel * group + plane * mine
            first = (c * ROWS + 1) * width
            cols[top : top + mine, first : first + ROWS * width] = jnp.zeros(
                (mine, ROWS * width), jnp.bfloat16
            )

    def compute(c):
        first = (c * ROWS + 1) * width
        right = cols[:, first : first + ROWS * width]
        for b in range(3):
            begin = (c * ROWS + b) * width
            part = lax.dot_general(
                source[:, begin : begin + ROWS * width],
                right,
                (((1,), (1,)), ((), ())),
                preferred_element_type=jnp.float32,
            )
            if c == 0:
                total[b] = part
            else:
                total[b] += part

    def compute_inputs(c):
        low = 0 if c == 0 else c * ROWS - 2
        high = height if c == chunks - 1 else (c + 1) * ROWS - 2
        for h in range(low, high, 2):
            stack = jnp.concatenate(
                [cols[:, (h + 2 - b) * width : (h + 4 - b) * width] for b in range(3)], axis=0
            )
            taps = jnp.concatenate([weights[b] for b in range(3)], axis=1)
            got = jnp.dot(taps, stack, preferred_element_type=jnp.float32)
            for i in range(2):
                span = slice(i * width, (i + 1) * width)
                for plane in range(2):
                    at = plane * mine
                    lo = got[at : at + mine, span]
                    mid = got[2 * mine + at : 2 * mine + at + mine, span]
                    hi = got[4 * mine + at : 4 * mine + at + mine, span]
                    value = (
                        mid
                        + jnp.where(lane < width - 1, pltpu.roll(lo, width - 1, 1), 0.0)
                        + jnp.where(lane > 0, pltpu.roll(hi, 1, 1), 0.0)
                    )
                    sums[plane, pl.ds(h + i, mine, stride=height), :] = value

    for plane in range(2):
        own_copy(plane).wait()

    def step(c):
        for rel in range(n_chan):
            for side in range(2):
                lay_halo(rel, side, c)
        compute(c)
        if c < chunks - 1:
            compute_inputs(c)

    for c in range(chunks):
        for plane in range(2):
            lay(0, plane + 1, c)
        for rel in range(1, n_chan):
            for plane in range(2):
                y_copy(n_chan - rel, plane, c).wait_recv()
            send_halo(rel, c)
            for plane in range(2):
                lay(rel, plane + 1, c)
        if c:
            step(c - 1)
    step(chunks - 1)

    blocks = n_space // n_chan
    keep = mine // blocks
    leave[...] = jnp.zeros_like(leave)
    for rel in range(n_chan):
        span = slice(rel * group, (rel + 1) * group)
        for b in range(3):
            for e in range(3):
                top = 2 * e * mine
                share = total[b, top : top + mine, span] + pltpu.roll(
                    total[b, top + mine : top + 2 * mine, span], group - mine, 1
                )
                share = share.astype(jnp.bfloat16)
                at = (3 * b + e) * keep
                for j in range(blocks):
                    leave[rel, j, at : at + keep, :] = share[j * keep : (j + 1) * keep]

    def share_copy(rel, j):
        return pltpu.make_async_remote_copy(
            src_ref=leave.at[rel, j],
            dst_ref=land.at[s],
            send_sem=s_send.at[rel, j],
            recv_sem=s_recv.at[s],
            device_id=(k * blocks + j, place(k, rel, n_chan)),
            device_id_type=pl.DeviceIdType.MESH,
        )

    def each_share(act, own):
        for rel in range(n_chan):
            for turn in range(blocks):
                j = lax.rem(turn + s, blocks)
                if rel == 0:
                    here = k * blocks + j == s

                    @pl.when(jnp.logical_not(here))
                    def _():
                        act(share_copy(rel, j))

                    @pl.when(here)
                    def _():
                        if own:
                            pltpu.make_async_copy(
                                leave.at[rel, j], land.at[s], s_recv.at[s]
                            ).start()

                else:
                    act(share_copy(rel, j))

    each_share(lambda d: d.start(), True)
    compute_inputs(chunks - 1)
    for plane in range(2):
        gi_ref[:, plane] = sums[plane].reshape(mine, height, width).astype(jnp.bfloat16)

    for i in range(n_space):
        pltpu.make_async_copy(land.at[i], land.at[i], s_recv.at[i]).wait()
    result = land[0].astype(jnp.float32)
    for i in range(1, n_space):
        result += land[i].astype(jnp.float32)
    gf_ref[...] = result

    each_share(lambda d: d.wait_send(), False)
    for c in range(chunks):
        for rel in range(1, n_chan):
            for plane in range(2):
                y_copy(rel, plane, c).wait_send()
        for rel in range(n_chan):

            @pl.when(below)
            def _():
                halo_copy(rel, 0, c).wait_send()

            @pl.when(above)
            def _():
                halo_copy(rel, 1, c).wait_send()


def fused(n_space, n_chan, inputs, grad_out, filt):
    mine, planes, height, width = inputs.shape
    keep = filt.shape[2] // n_space
    blocks = n_space // n_chan
    taps = filt.reshape(3, 3, 3, mine, n_chan, mine)[::-1].transpose(4, 1, 2, 5, 0, 3)
    taps = taps.reshape(n_chan, 9 * mine, 3 * mine)
    taps = jnp.pad(taps, ((0, 0), (0, 0), (0, mine)))
    share_rows = -(-9 * keep // 16) * 16
    chunks = height // ROWS
    group = 4 * mine
    dma = pltpu.SemaphoreType.DMA
    vmem = pl.BlockSpec(memory_space=pltpu.VMEM)
    grad_inputs, share = pl.pallas_call(
        functools.partial(body, n_space, n_chan),
        out_shape=(
            jax.ShapeDtypeStruct(inputs.shape, jnp.bfloat16),
            jax.ShapeDtypeStruct((share_rows, group), jnp.float32),
        ),
        in_specs=[vmem, vmem, pl.BlockSpec(memory_space=pl.ANY)],
        out_specs=(vmem, vmem),
        scratch_shapes=[
            pltpu.VMEM((n_chan, 4, mine, height, width), jnp.bfloat16),
            pltpu.VMEM((n_chan * group, (height + 2) * width), jnp.bfloat16),
            pltpu.VMEM((6 * mine, (height + 2) * width), jnp.bfloat16),
            pltpu.VMEM((mine * ROWS, width), jnp.float32),
            pltpu.VMEM((3, 6 * mine, n_chan * group), jnp.float32),
            pltpu.VMEM((3, 6 * mine, n_chan * group), jnp.bfloat16),
            pltpu.VMEM((n_chan, 9 * mine, group), jnp.bfloat16),
            pltpu.VMEM((2, mine * height, width), jnp.float32),
            pltpu.VMEM((n_chan, blocks, share_rows, group), jnp.bfloat16),
            pltpu.VMEM((n_space, share_rows, group), jnp.bfloat16),
            dma((2,)),
            dma((n_chan - 1, 2, chunks)),
            dma((n_chan, 2, chunks)),
            dma((n_chan, 4, chunks)),
            dma((n_chan - 1,)),
            dma((n_chan - 1,)),
            dma((n_chan, blocks)),
            dma((n_space,)),
        ],
        compiler_params=pltpu.CompilerParams(has_side_effects=True, vmem_limit_bytes=56 << 20),
    )(taps, inputs, grad_out)
    share = share[: 9 * keep].reshape(9, keep, 4, mine)[:, :, 2::-1]
    return grad_inputs, share.transpose(2, 0, 3, 1).reshape(27, mine, keep)


def solution(mesh):
    n_space, n_chan = mesh.shape["space"], mesh.shape["chan"]

    def run(inputs, grad_out, filt):
        mine, planes, height, width = inputs.shape
        fits = (
            planes == 2
            and n_chan > 1
            and width == 128
            and 4 * mine == width
            and grad_out.shape[0] == mine
            and filt.shape[2] == n_chan * mine
            and height % ROWS == 0
            and n_space % n_chan == 0
            and filt.shape[2] % n_space == 0
        )
        if fits:
            return fused(n_space, n_chan, inputs, grad_out, filt)
        return local(inputs, grad_out, filt)

    return jax.shard_map(
        run,
        mesh=mesh,
        in_specs=(
            P("chan", "space", None, None),
            P("chan", "space", None, None),
            P(None, "chan", None),
        ),
        out_specs=(P("chan", "space", None, None), P(None, "chan", "space")),
        check_vma=False,
    )
```

profile of v0, /device:TPU:5, one launch (start us, length us, event | category | flops | bytes accessed | tf_op | source)
XLA Modules:
  0.0 61.9 jit_solution(14306910302063062624)
XLA Ops:
  0.6 1.1 %reshape.16 = bf16[3,3,3,32,2,32]{5,4,3,2,1,0:T(2,128)(2,1)S(1)} reshape(bf16[27,32,64]{2,1,0:T(8,128)(2,1)} %param.5) | data formatting | bytes 221184 | tf_op jit(solution)/shard_map/reshape | solution.py:405
  1.8 0.6 copy.7
  2.4 1.6 %rev.6 = bf16[3,3,3,32,2,32]{3,0,5,2,1,4:T(4,128)(2,1)S(1)} reverse(bf16[3,3,3,32,2,32]{3,0,5,2,1,4:T(4,128)(2,1)S(1)} %copy.7), dimensions={0} | reverse | bytes 221184 | tf_op jit(solution)/shard_map/rev | solution.py:405
  4.0 0.3 reshape.17
  4.3 0.7 %pad.4.filt_ref = bf16[2,288,128]{2,1,0:T(8,128)(2,1)} pad(bf16[2,288,96]{2,1,0:T(8,128)(2,1)S(1)} %reshape.17, bf16[]{:T(256)} %constant.2.clone.1), padding=0_0x0_0x0_32 | pad | bytes 258050 | tf_op jit(solution)/shard_map/jit(_pad)/pad | solution.py:407
  4.9 53.1 %shard_map.50 = (bf16[32,2,64,128]{3,2,1,0:T(8,128)(2,1)}, f32[48,128]{1,0:T(8,128)}) custom-call(bf16[2,288,128]{2,1,0:T(8,128)(2,1)} %pad.4.filt_ref, bf16[32,2,64,128]{3,2,1,0:T(8,128)(2,1)} %in_ref.1, bf16[32,2,64,128]{3,2,1,0:T(8,128)(2,1)} %out_hbm.1), custom_call_target="tpu_custom_call" | custom-call | tf_op jit(solution)/shard_map/pallas_call | solution.py:413
  58.0 0.7 %slice.6 = f32[36,128]{1,0:T(8,128)S(1)} slice(f32[48,128]{1,0:T(8,128)} %get-tuple-element.5), slice={[0:36], [0:128]} | slice | bytes 36864 | tf_op jit(solution)/shard_map/slice | solution.py:443
  58.8 0.1 reshape.18
  58.9 0.1 rev.7
  58.9 0.6 %copy.8 = f32[3,9,32,4]{2,3,1,0:T(4,128)} copy(f32[3,9,32,4]{2,0,3,1:T(4,128)S(1)} %bitcast.6) | data formatting | bytes 27648 | tf_op jit(solution)/shard_map/transpose | solution.py:444
  59.6 2.3 %copy.10 = bf16[32,2,64,128]{3,2,1,0:T(8,128)(2,1)} copy(bf16[32,2,64,128]{3,2,1,0:T(8,128)(2,1)} %get-tuple-element.8) | data formatting | bytes 2097152
where the time goes:
time: 62.2 us; the launch traced here: 61.9 us
  Pallas kernels  53.1 us (85%)
  local copies, waits for them, and re-layouts  8.14 us (13%)
  between operations  0.68 us (1%)
    pallas_call x1, Pallas kernels, fused(): pl.pallas_call(functools.partial(body, n_space, n_chan), out_shape=(jax.S...  53.1 us
    unnamed x1, local copies, waits for them, and re-layouts  2.3 us
    reshape x2, local copies, waits for them, and re-layouts, fused(): filt.reshape(3, 3, 3, mine, n_chan, mine)[::-1].transpose(4, 1, 2, 5, 0, 3)  1.75 us
    rev x1, local copies, waits for them, and re-layouts, fused(): filt.reshape(3, 3, 3, mine, n_chan, mine)[::-1].transpose(4, 1, 2, 5, 0, 3)  1.59 us

commit v1 on v0

--- a/solution.py
+++ b/solution.py
@@ -95,7 +95,7 @@
     n_space,
     n_chan,
     filt_ref,
-    in_ref,
+    in_hbm,
     out_hbm,
     gi_ref,
     gf_ref,
@@ -105,11 +105,14 @@
     held,
     total,
     weights,
+    in_ref,
+    my_filt,
     their_filt,
     sums,
     leave,
     land,
     own_sem,
+    in_sem,
     y_send,
     h_send,
     arrive,
@@ -124,6 +127,8 @@
     group = 4 * mine
     s = lax.axis_index("space")
     k = lax.axis_index("chan")
+    edge = lax.rem(s, 2)
+    inner = 1 - edge
     lane = lax.broadcasted_iota(jnp.int32, (mine, width), 1)
 
     def rows_of(c):
@@ -157,7 +162,7 @@
 
     def filt_copy(rel):
         return pltpu.make_async_remote_copy(
-            src_ref=filt_ref.at[place(k, rel, n_chan)],
+            src_ref=my_filt.at[place(k, rel, n_chan)],
             dst_ref=their_filt.at[n_chan - rel],
             send_sem=f_send.at[rel - 1],
             recv_sem=f_recv.at[n_chan - rel - 1],
@@ -181,15 +186,33 @@
         def _():
             halo_copy(rel, 1, c).start()
 
+    def start_y(plane, c):
+        for rel in range(1, n_chan):
+            y_copy(rel, plane, c).start()
+
+    load = pltpu.make_async_copy(in_hbm, in_ref, in_sem.at[0])
+    start_y(edge, 0)
+    load.start()
+    for plane in range(2):
+        own_copy(plane).start()
+    for c in range(chunks):
+        send_halo(0, c)
+
+    for b in range(3):
+        for e in range(3):
+            taps = [filt_ref[9 * (2 - p) + 3 * b + e].astype(jnp.float32) for p in range(3)]
+            turned = jnp.concatenate(taps + [jnp.zeros_like(taps[0])], axis=0).T
+            at = (3 * b + e) * mine
+            for part in range(n_chan):
+                my_filt[part, at : at + mine, :] = turned[
+                    part * mine : (part + 1) * mine
+                ].astype(jnp.bfloat16)
     for rel in range(1, n_chan):
         filt_copy(rel).start()
     for c in range(chunks):
-        for rel in range(1, n_chan):
-            for plane in range(2):
-                y_copy(rel, plane, c).start()
-        send_halo(0, c)
-    for plane in range(2):
-        own_copy(plane).start()
+        if c < chunks - 1:
+            start_y(edge, c + 1)
+        start_y(inner, c)
 
     pad = jnp.zeros((source.shape[0], width), jnp.bfloat16)
     source[:, 0:width] = pad
@@ -213,6 +236,7 @@
                     source[top : top + mine, at] = value.astype(jnp.bfloat16)
         return carry
 
+    load.wait()
     lax.fori_loop(0, chunks, source_step, 0)
 
     def set_weights(rel, value):
@@ -228,7 +252,7 @@
                     jnp.bfloat16
                 )
 
-    set_weights(0, filt_ref[k])
+    set_weights(0, my_filt[k])
     for rel in range(1, n_chan):
         filt_copy(rel).wait()
     for rel in range(1, n_chan):
@@ -260,9 +284,9 @@
                 (mine, ROWS * width), jnp.bfloat16
             )
 
-    def compute(c):
+    def compute(rel, c):
         first = (c * ROWS + 1) * width
-        right = cols[:, first : first + ROWS * width]
+        right = cols[rel * group : (rel + 1) * group, first : first + ROWS * width]
         for b in range(3):
             begin = (c * ROWS + b) * width
             part = lax.dot_general(
@@ -272,9 +296,9 @@
                 preferred_element_type=jnp.float32,
             )
             if c == 0:
-                total[b] = part
+                total[rel, b] = part
             else:
-                total[b] += part
+                total[rel, b] += part
 
     def compute_inputs(c):
         low = 0 if c == 0 else c * ROWS - 2
@@ -299,40 +323,48 @@
                     )
                     sums[plane, pl.ds(h + i, mine, stride=height), :] = value
 
-    for plane in range(2):
-        own_copy(plane).wait()
-
-    def step(c):
-        for rel in range(n_chan):
+    def round_rows(c):
+        first = c * ROWS
+        for plane in range(2):
+            for i in range(mine):
+                value = sums[plane, i * height + first : i * height + first + ROWS, :]
+                gi_ref[i, plane, first : first + ROWS, :] = value.astype(jnp.bfloat16)
+
+    def lay_own(c):
+        for plane in range(2):
+            lay(0, plane + 1, c)
+        for side in range(2):
+            lay_halo(0, side, c)
+        compute(0, c)
+
+    def finish(c):
+        for rel in range(1, n_chan):
             for side in range(2):
                 lay_halo(rel, side, c)
-        compute(c)
-        if c < chunks - 1:
-            compute_inputs(c)
-
-    for c in range(chunks):
-        for plane in range(2):
-            lay(0, plane + 1, c)
+            compute(rel, c)
+
+    def forward(plane, c):
         for rel in range(1, n_chan):
-            for plane in range(2):
-                y_copy(n_chan - rel, plane, c).wait_recv()
-            send_halo(rel, c)
-            for plane in range(2):
-                lay(rel, plane + 1, c)
-        if c:
-            step(c - 1)
-    step(chunks - 1)
+            y_copy(n_chan - rel, plane, c).wait_recv()
+
+            @pl.when(jnp.logical_and(plane == 0, below))
+            def _():
+                halo_copy(rel, 0, c).start()
+
+            @pl.when(jnp.logical_and(plane == 1, above))
+            def _():
+                halo_copy(rel, 1, c).start()
 
     blocks = n_space // n_chan
     keep = mine // blocks
     leave[...] = jnp.zeros_like(leave)
-    for rel in range(n_chan):
-        span = slice(rel * group, (rel + 1) * group)
+
+    def fill_share(rel):
         for b in range(3):
             for e in range(3):
                 top = 2 * e * mine
-                share = total[b, top : top + mine, span] + pltpu.roll(
-                    total[b, top + mine : top + 2 * mine, span], group - mine, 1
+                share = total[rel, b, top : top + mine, :] + pltpu.roll(
+                    total[rel, b, top + mine : top + 2 * mine, :], group - mine, 1
                 )
                 share = share.astype(jnp.bfloat16)
                 at = (3 * b + e) * keep
@@ -349,31 +381,54 @@
             device_id_type=pl.DeviceIdType.MESH,
         )
 
-    def each_share(act, own):
-        for rel in range(n_chan):
-            for turn in range(blocks):
-                j = lax.rem(turn + s, blocks)
-                if rel == 0:
-                    here = k * blocks + j == s
-
-                    @pl.when(jnp.logical_not(here))
-                    def _():
-                        act(share_copy(rel, j))
+    def each_share(rel, act, own):
+        for turn in range(blocks):
+            j = lax.rem(turn + s, blocks)
+            if rel == 0:
+                here = k * blocks + j == s
+
+                @pl.when(jnp.logical_not(here))
+                def _():
+                    act(share_copy(rel, j))
+
+                if own:
 
                     @pl.when(here)
                     def _():
-                        if own:
-                            pltpu.make_async_copy(
-                                leave.at[rel, j], land.at[s], s_recv.at[s]
-                            ).start()
-
-                else:
-                    act(share_copy(rel, j))
-
-    each_share(lambda d: d.start(), True)
+                        pltpu.make_async_copy(leave.at[rel, j], land.at[s], s_recv.at[s]).start()
+
+            else:
+                act(share_copy(rel, j))
+
+    def send_share(rel):
+        fill_share(rel)
+        each_share(rel, lambda d: d.start(), True)
+
+    for plane in range(2):
+        own_copy(plane).wait()
+    forward(edge, 0)
+    for c in range(chunks):
+        if c < chunks - 1:
+            forward(edge, c + 1)
+            lay_own(c)
+        if c == chunks - 2:
+            lay_own(chunks - 1)
+            send_share(0)
+        if c:
+            finish(c - 1)
+            compute_inputs(c - 1)
+            if c > 1:
+                round_rows(c - 2)
+        forward(inner, c)
+        for rel in range(1, n_chan):
+            for plane in range(2):
+                lay(rel, plane + 1, c)
+    finish(chunks - 1)
+    for rel in range(1, n_chan):
+        send_share(rel)
     compute_inputs(chunks - 1)
-    for plane in range(2):
-        gi_ref[:, plane] = sums[plane].reshape(mine, height, width).astype(jnp.bfloat16)
+    for c in range(max(chunks - 2, 0), chunks):
+        round_rows(c)
 
     for i in range(n_space):
         pltpu.make_async_copy(land.at[i], land.at[i], s_recv.at[i]).wait()
@@ -382,7 +437,8 @@
         result += land[i].astype(jnp.float32)
     gf_ref[...] = result
 
-    each_share(lambda d: d.wait_send(), False)
+    for rel in range(n_chan):
+        each_share(rel, lambda d: d.wait_send(), False)
     for c in range(chunks):
         for rel in range(1, n_chan):
             for plane in range(2):
@@ -402,9 +458,6 @@
     mine, planes, height, width = inputs.shape
     keep = filt.shape[2] // n_space
     blocks = n_space // n_chan
-    taps = filt.reshape(3, 3, 3, mine, n_chan, mine)[::-1].transpose(4, 1, 2, 5, 0, 3)
-    taps = taps.reshape(n_chan, 9 * mine, 3 * mine)
-    taps = jnp.pad(taps, ((0, 0), (0, 0), (0, mine)))
     share_rows = -(-9 * keep // 16) * 16
     chunks = height // ROWS
     group = 4 * mine
@@ -416,20 +469,23 @@
             jax.ShapeDtypeStruct(inputs.shape, jnp.bfloat16),
             jax.ShapeDtypeStruct((share_rows, group), jnp.float32),
         ),
-        in_specs=[vmem, vmem, pl.BlockSpec(memory_space=pl.ANY)],
+        in_specs=[vmem, pl.BlockSpec(memory_space=pl.ANY), pl.BlockSpec(memory_space=pl.ANY)],
         out_specs=(vmem, vmem),
         scratch_shapes=[
             pltpu.VMEM((n_chan, 4, mine, height, width), jnp.bfloat16),
             pltpu.VMEM((n_chan * group, (height + 2) * width), jnp.bfloat16),
             pltpu.VMEM((6 * mine, (height + 2) * width), jnp.bfloat16),
             pltpu.VMEM((mine * ROWS, width), jnp.float32),
-            pltpu.VMEM((3, 6 * mine, n_chan * group), jnp.float32),
+            pltpu.VMEM((n_chan, 3, 6 * mine, group), jnp.float32),
             pltpu.VMEM((3, 6 * mine, n_chan * group), jnp.bfloat16),
+            pltpu.VMEM(inputs.shape, jnp.bfloat16),
+            pltpu.VMEM((n_chan, 9 * mine, group), jnp.bfloat16),
             pltpu.VMEM((n_chan, 9 * mine, group), jnp.bfloat16),
             pltpu.VMEM((2, mine * height, width), jnp.float32),
             pltpu.VMEM((n_chan, blocks, share_rows, group), jnp.bfloat16),
             pltpu.VMEM((n_space, share_rows, group), jnp.bfloat16),
             dma((2,)),
+            dma((1,)),
             dma((n_chan - 1, 2, chunks)),
             dma((n_chan, 2, chunks)),
             dma((n_chan, 4, chunks)),
@@ -438,8 +494,8 @@
             dma((n_chan, blocks)),
             dma((n_space,)),
         ],
-        compiler_params=pltpu.CompilerParams(has_side_effects=True, vmem_limit_bytes=56 << 20),
-    )(taps, inputs, grad_out)
+        compiler_params=pltpu.CompilerParams(has_side_effects=True, vmem_limit_bytes=24 << 20),
+    )(filt, inputs, grad_out)
     share = share[: 9 * keep].reshape(9, keep, 4, mine)[:, :, 2::-1]
     return grad_inputs, share.transpose(2, 0, 3, 1).reshape(27, mine, keep)
 

time: 62.2 us -> 52.9 us (0.85)
  Pallas kernels: 53.1 us -> 46.9 us
  local copies, waits for them, and re-layouts: 8.14 us -> 5.17 us
    pallas_call x1, Pallas kernels: 53.1 us -> 46.9 us  [fused(): pl.pallas_call(functools.partial(body, n_space, n_chan), out_shape=(jax.S...]
    unnamed x1 -> x7, local copies, waits for them, and re-layouts: 2.3 us -> 4.35 us
    reshape x3 -> x0, local copies, waits for them, and re-layouts: 2.01 us -> none  [the longest x2 1.75 us: fused(): filt.reshape(3, 3, 3, mine, n_chan, mine)[::-1].transpose(4, 1, 2, 5, 0, 3)]
    rev x1 -> x0, local copies, waits for them, and re-layouts: 1.59 us -> none  [fused(): filt.reshape(3, 3, 3, mine, n_chan, mine)[::-1].transpose(4, 1, 2, 5, 0, 3)]
    slice x1, local copies, waits for them, and re-layouts: 0.73 us -> 0.01 us  [fused(): share = share[:9 * keep].reshape(9, keep, 4, mine)[:, :, 2::-1]]
    pad x1 -> x0, local copies, waits for them, and re-layouts: 0.7 us -> none  [fused(): taps = jnp.pad(taps, ((0, 0), (0, 0), (0, mine)))]
where the time goes in v1:
time: 52.9 us; the launch traced here: 52.7 us
  Pallas kernels  46.9 us (89%)
  local copies, waits for them, and re-layouts  5.17 us (10%)
  between operations  0.67 us (1%)
    pallas_call x1, Pallas kernels, fused(): pl.pallas_call(functools.partial(body, n_space, n_chan), out_shape=(jax.S...  46.9 us
    unnamed x7, local copies, waits for them, and re-layouts  4.35 us

profile of v1, /device:TPU:5, one launch (start us, length us, event | category | flops | bytes accessed | tf_op | source)
XLA Modules:
  0.0 52.7 jit_solution(694631069354094174)
XLA Ops:
  0.6 0.0 copy-start
  0.6 1.2 %copy-done = bf16[32,2,64,128]{3,2,1,0:T(8,128)(2,1)S(1)} copy-done((bf16[32,2,64,128]{3,2,1,0:T(8,128)(2,1)S(1)}, bf16[32,2,64,128]{3,2,1,0:T(8,128)(2,1)}, u32[]{:S(2)}) %copy-start) | copy-done | bytes 1048600
  1.9 0.0 copy-start.1
  1.9 1.2 %copy-done.1 = bf16[32,2,64,128]{3,2,1,0:T(8,128)(2,1)S(1)} copy-done((bf16[32,2,64,128]{3,2,1,0:T(8,128)(2,1)S(1)}, bf16[32,2,64,128]{3,2,1,0:T(8,128)(2,1)}, u32[]{:S(2)}) %copy-start.1) | copy-done | bytes 1048600
  3.1 0.0 copy-start.2
  3.1 0.9 %copy-done.2 = bf16[27,32,64]{2,1,0:T(8,128)(2,1)S(1)} copy-done((bf16[27,32,64]{2,1,0:T(8,128)(2,1)S(1)}, bf16[27,32,64]{2,1,0:T(8,128)(2,1)}, u32[]{:S(2)}) %copy-start.2) | copy-done | bytes 110616
  4.0 46.9 %shard_map.50 = (bf16[32,2,64,128]{3,2,1,0:T(8,128)(2,1)S(1)}, f32[48,128]{1,0:T(8,128)S(1)}) custom-call(bf16[27,32,64]{2,1,0:T(8,128)(2,1)S(1)} %copy-done.2, bf16[32,2,64,128]{3,2,1,0:T(8,128)(2,1)S(1)} %copy-done, bf16[32,2,64,128]{3,2,1,0:T(8,128)(2,1)S(1)} %copy-done.1), custom_call_target="tpu_custom_call" | custom-call | tf_op jit(solution)/shard_map/pallas_call | solution.py:466
  50.9 0.1 reshape.10
  51.0 0.1 rev.3
  51.1 0.6 %copy.5 = f32[3,9,32,4]{2,3,1,0:T(4,128)} copy(f32[3,9,32,4]{2,0,3,1:T(4,128)S(1)} %bitcast.4) | data formatting | bytes 27648 | tf_op jit(solution)/shard_map/transpose | solution.py:500
  51.8 1.0 %copy.7 = bf16[32,2,64,128]{3,2,1,0:T(8,128)(2,1)} copy(bf16[32,2,64,128]{3,2,1,0:T(8,128)(2,1)S(1)} %get-tuple-element.8) | data formatting | bytes 2097152
  (1 shorter events, 0.0 us)
Async XLA Ops:
  0.6 1.2 %copy-start = (bf16[32,2,64,128]{3,2,1,0:T(8,128)(2,1)S(1)}, bf16[32,2,64,128]{3,2,1,0:T(8,128)(2,1)}, u32[]{:S(2)}) copy-start(bf16[32,2,64,128]{3,2,1,0:T(8,128)(2,1)} %in_hbm.1) | copy-start | bytes 3145732
  1.9 1.2 %copy-start.1 = (bf16[32,2,64,128]{3,2,1,0:T(8,128)(2,1)S(1)}, bf16[32,2,64,128]{3,2,1,0:T(8,128)(2,1)}, u32[]{:S(2)}) copy-start(bf16[32,2,64,128]{3,2,1,0:T(8,128)(2,1)} %out_hbm.1) | copy-start | bytes 3145732
  3.1 0.9 %copy-start.2 = (bf16[27,32,64]{2,1,0:T(8,128)(2,1)S(1)}, bf16[27,32,64]{2,1,0:T(8,128)(2,1)}, u32[]{:S(2)}) copy-start(bf16[27,32,64]{2,1,0:T(8,128)(2,1)} %filt_ref.1) | copy-start | bytes 331780

commit v2 on v1

--- a/solution.py
+++ b/solution.py
@@ -94,7 +94,7 @@
 def body(
     n_space,
     n_chan,
-    filt_ref,
+    filt_hbm,
     in_hbm,
     out_hbm,
     gi_ref,
@@ -106,6 +106,7 @@
     total,
     weights,
     in_ref,
+    filt_ref,
     my_filt,
     their_filt,
     sums,
@@ -120,6 +121,7 @@
     f_recv,
     s_send,
     s_recv,
+    met,
 ):
     mine = in_ref.shape[0]
     height, width = in_ref.shape[2], in_ref.shape[3]
@@ -130,6 +132,10 @@
     edge = lax.rem(s, 2)
     inner = 1 - edge
     lane = lax.broadcasted_iota(jnp.int32, (mine, width), 1)
+
+    def partner(b):
+        bit = 1 << b
+        return s + bit - 2 * bit * lax.rem(s // bit, 2)
 
     def rows_of(c):
         return pl.ds(c * ROWS, ROWS)
@@ -186,18 +192,61 @@
         def _():
             halo_copy(rel, 1, c).start()
 
+    rounds = n_space.bit_length() - 1
+    mesh_id = pl.DeviceIdType.MESH
+    barrier = pltpu.get_barrier_semaphore()
+    for b in range(rounds):
+        pl.semaphore_signal(
+            barrier, inc=1, device_id=(partner(b), k), device_id_type=mesh_id
+        )
+    for rel in range(1, n_chan):
+        pl.semaphore_signal(
+            barrier, inc=1, device_id=(s, place(k, rel, n_chan)), device_id_type=mesh_id
+        )
+
+    @pl.when(jnp.logical_and(edge == 0, below))
+    def _():
+        pl.semaphore_signal(barrier, inc=1, device_id=(s - 1, k), device_id_type=mesh_id)
+
+    @pl.when(jnp.logical_and(edge == 1, above))
+    def _():
+        pl.semaphore_signal(barrier, inc=1, device_id=(s + 1, k), device_id_type=mesh_id)
+
+    beside = jnp.where(edge == 0, s > 0, s < n_space - 1).astype(jnp.int32)
+    pl.semaphore_wait(barrier, rounds + n_chan - 1 + beside)
+
+    def advance(i):
+        if i > 0:
+            pl.semaphore_wait(met.at[i - 1], 1 if i <= rounds else n_chan - 1)
+        if i < rounds:
+            pl.semaphore_signal(
+                met.at[i], inc=1, device_id=(partner(i), k), device_id_type=mesh_id
+            )
+        elif i == rounds:
+            for rel in range(1, n_chan):
+                pl.semaphore_signal(
+                    met.at[i],
+                    inc=1,
+                    device_id=(s, place(k, rel, n_chan)),
+                    device_id_type=mesh_id,
+                )
+
     def start_y(plane, c):
         for rel in range(1, n_chan):
             y_copy(rel, plane, c).start()
 
     load = pltpu.make_async_copy(in_hbm, in_ref, in_sem.at[0])
     start_y(edge, 0)
+    load_filt = pltpu.make_async_copy(filt_hbm, filt_ref, in_sem.at[1])
+    load_filt.start()
     load.start()
     for plane in range(2):
         own_copy(plane).start()
     for c in range(chunks):
         send_halo(0, c)
 
+    advance(0)
+    load_filt.wait()
     for b in range(3):
         for e in range(3):
             taps = [filt_ref[9 * (2 - p) + 3 * b + e].astype(jnp.float32) for p in range(3)]
@@ -213,6 +262,7 @@
         if c < chunks - 1:
             start_y(edge, c + 1)
         start_y(inner, c)
+    advance(1)
 
     pad = jnp.zeros((source.shape[0], width), jnp.bfloat16)
     source[:, 0:width] = pad
@@ -238,6 +288,7 @@
 
     load.wait()
     lax.fori_loop(0, chunks, source_step, 0)
+    advance(2)
 
     def set_weights(rel, value):
         taps = value.astype(jnp.float32)
@@ -257,6 +308,8 @@
         filt_copy(rel).wait()
     for rel in range(1, n_chan):
         set_weights(rel, their_filt[rel])
+
+    advance(3)
 
     def lay(rel, plane, c):
         block = raw[rel, plane, :, rows_of(c), :].astype(jnp.float32)
@@ -411,8 +464,12 @@
         if c < chunks - 1:
             forward(edge, c + 1)
             lay_own(c)
+        if c == 0:
+            for i in range(4, rounds + 1):
+                advance(i)
         if c == chunks - 2:
             lay_own(chunks - 1)
+            advance(rounds + 1)
             send_share(0)
         if c:
             finish(c - 1)
@@ -463,13 +520,15 @@
     group = 4 * mine
     dma = pltpu.SemaphoreType.DMA
     vmem = pl.BlockSpec(memory_space=pltpu.VMEM)
+    rounds = n_space.bit_length() - 1
+    hbm = pl.BlockSpec(memory_space=pltpu.HBM)
     grad_inputs, share = pl.pallas_call(
         functools.partial(body, n_space, n_chan),
         out_shape=(
             jax.ShapeDtypeStruct(inputs.shape, jnp.bfloat16),
             jax.ShapeDtypeStruct((share_rows, group), jnp.float32),
         ),
-        in_specs=[vmem, pl.BlockSpec(memory_space=pl.ANY), pl.BlockSpec(memory_space=pl.ANY)],
+        in_specs=[hbm, hbm, hbm],
         out_specs=(vmem, vmem),
         scratch_shapes=[
             pltpu.VMEM((n_chan, 4, mine, height, width), jnp.bfloat16),
@@ -479,13 +538,14 @@
             pltpu.VMEM((n_chan, 3, 6 * mine, group), jnp.float32),
             pltpu.VMEM((3, 6 * mine, n_chan * group), jnp.bfloat16),
             pltpu.VMEM(inputs.shape, jnp.bfloat16),
+            pltpu.VMEM(filt.shape, jnp.bfloat16),
             pltpu.VMEM((n_chan, 9 * mine, group), jnp.bfloat16),
             pltpu.VMEM((n_chan, 9 * mine, group), jnp.bfloat16),
             pltpu.VMEM((2, mine * height, width), jnp.float32),
             pltpu.VMEM((n_chan, blocks, share_rows, group), jnp.bfloat16),
             pltpu.VMEM((n_space, share_rows, group), jnp.bfloat16),
             dma((2,)),
-            dma((1,)),
+            dma((2,)),
             dma((n_chan - 1, 2, chunks)),
             dma((n_chan, 2, chunks)),
             dma((n_chan, 4, chunks)),
@@ -493,9 +553,10 @@
             dma((n_chan - 1,)),
             dma((n_chan, blocks)),
             dma((n_space,)),
+            pltpu.SemaphoreType.REGULAR((rounds + 1,)),
         ],
-        compiler_params=pltpu.CompilerParams(has_side_effects=True, vmem_limit_bytes=24 << 20),
-    )(filt, inputs, grad_out)
+        compiler_params=pltpu.CompilerParams(has_side_effects=True, collective_id=0, vmem_limit_bytes=24 << 20),
+    )(*(pltpu.with_memory_space_constraint(x, pltpu.HBM) for x in (filt, inputs, grad_out)))
     share = share[: 9 * keep].reshape(9, keep, 4, mine)[:, :, 2::-1]
     return grad_inputs, share.transpose(2, 0, 3, 1).reshape(27, mine, keep)
 
@@ -514,6 +575,9 @@
             and filt.shape[2] == n_chan * mine
             and height % ROWS == 0
             and n_space % n_chan == 0
+            and n_space & (n_space - 1) == 0
+            and n_space >= 8
+            and height // ROWS >= 3
             and filt.shape[2] % n_space == 0
         )
         if fits:

time: 52.9 us -> 46.1 us (0.87)
  Pallas kernels: 46.9 us -> 43.5 us
  local copies, waits for them, and re-layouts: 5.17 us -> 1.79 us
    unnamed x7 -> x1, local copies, waits for them, and re-layouts: 4.35 us -> 0.97 us
    pallas_call x1, Pallas kernels: 46.9 us -> 43.5 us  [fused(): pl.pallas_call(functools.partial(body, n_space, n_chan), out_shape=(jax.S...]
where the time goes in v2:
time: 46.1 us; the launch traced here: 46 us
  Pallas kernels  43.5 us (94%)
  local copies, waits for them, and re-layouts  1.79 us (4%)
  between operations  0.66 us (1%)
    pallas_call x1, Pallas kernels, fused(): pl.pallas_call(functools.partial(body, n_space, n_chan), out_shape=(jax.S...  43.5 us
    unnamed x1, local copies, waits for them, and re-layouts  0.97 us

profile of v2, /device:TPU:5, one launch (start us, length us, event | category | flops | bytes accessed | tf_op | source)
XLA Modules:
  0.0 46.0 jit_solution(14376491511200146758)
XLA Ops:
  0.6 43.5 %shard_map.50 = (bf16[32,2,64,128]{3,2,1,0:T(8,128)(2,1)S(1)}, f32[48,128]{1,0:T(8,128)S(1)}) custom-call(bf16[27,32,64]{2,1,0:T(8,128)(2,1)} %filt_hbm.1, bf16[32,2,64,128]{3,2,1,0:T(8,128)(2,1)} %in_hbm.1, bf16[32,2,64,128]{3,2,1,0:T(8,128)(2,1)} %out_hbm.1), custom_call_target="tpu_custom_call" | custom-call | tf_op jit(solution)/shard_map/pallas_call | solution.py:525
  44.2 0.1 reshape.10
  44.3 0.1 rev.3
  44.4 0.6 %copy.5 = f32[3,9,32,4]{2,3,1,0:T(4,128)} copy(f32[3,9,32,4]{2,0,3,1:T(4,128)S(1)} %bitcast.4) | data formatting | bytes 27648 | tf_op jit(solution)/shard_map/transpose | solution.py:561
  45.0 1.0 %copy.7 = bf16[32,2,64,128]{3,2,1,0:T(8,128)(2,1)} copy(bf16[32,2,64,128]{3,2,1,0:T(8,128)(2,1)S(1)} %get-tuple-element.8) | data formatting | bytes 2097152
  (1 shorter events, 0.0 us)
